TPU v7x, 32 devices: a whole 2x2x4 slice. The times are simulated.
32 devices in a mesh: seq: 8 (over z, x), tensor: 4 (over y, core).
Axes of the slice: x: 2, y: 2, z: 4, core: 2. Of those that a mesh axis runs over, the one named last changes fastest.
Arguments:
- hidden_in: bfloat16 [16, 5120], replicated, may hold values from -6 to 6
- united_down: bfloat16 [5120, 2112], P(None, 'tensor'), may hold values from -0.078125 to 0.078125
- q_gain: float32 [1536], replicated, may hold values from 0.1 to 1.9
- kv_gain: float32 [512], replicated, may hold values from 0.1 to 1.9
- q_up: bfloat16 [1536, 24576], P('seq', 'tensor'), may hold values from -0.15625 to 0.15625
- key_up: bfloat16 [512, 16384], P(None, 'tensor'), may hold values from -0.25 to 0.25
- value_up: bfloat16 [512, 16384], P(None, 'tensor'), may hold values from -0.0625 to 0.0625
- latent_block_store: bfloat16 [512, 128, 512], P(('seq', 'tensor')), may hold values from -24 to 24
- rope_pool: bfloat16 [512, 64, 128], P(('seq', 'tensor')), may hold values from -124 to 124
- lengths: int32 [16], replicated, may hold values from 2048 to 4096, as said below
- block_table: int32 [16, 32], P(None, 'seq'), may hold values from 0 to 511, as said below
Outputs:
- attn_out: bfloat16 [16, 16384], P(None, 'tensor')
- new_entry: bfloat16 [16, 576], replicated
Inputs may be any that keep to these rules, and one draw needn't show every extreme that they name: `lengths`: every sequence holds 2048 to 4096 cached positions; one sequence holds exactly 4096 and another exactly 2048. block_table[b, j] is the pool slot of positions j * 128 to (j + 1) * 128 - 1 of sequence b. The columns j with j // 4 = s name exactly the 64 slots s * 16 * 4 to (s + 1) * 16 * 4 - 1, each once, in any order; blocks past a sequence's length also name such slots.
All inputs are finite; a program needn't handle non-finite values.
Results may differ from a plain program's by a relative error of at most 0.015.
The roundings to bfloat16 on the way count: a program that leaves them out, or rounds other values in their place, can miss the bound.
Values may be sent and summed in bfloat16 or wider, within the bound.
A program may use at most 128 MiB of HBM per device.

v0:
```python
import jax
import jax.numpy as jnp
from jax import lax
from jax.sharding import PartitionSpec as P

QR = 1536
LATENT_RANK = 512
NOPE = 128
VD = 128
B = 16
BLOCK_POSITIONS = 128
QH = 192
NORM_FLOOR = 1.0
FLOOR_SCORE = -1e30


def rms_scale(row_values, gain_row):
    mean_square = jnp.mean(row_values * row_values, axis=-1, keepdims=True)
    return row_values * lax.rsqrt(mean_square + NORM_FLOOR) * gain_row


def rotate_pairs(rope_pairs, positions):
    half_dim = rope_pairs.shape[-1] // 2
    inverse_freq = 10000.0 ** (
        -2.0 * jnp.arange(half_dim, dtype=jnp.float32) / rope_pairs.shape[-1]
    )
    angles = positions[..., None] * inverse_freq
    cosine = jnp.cos(angles)
    sine_part = jnp.sin(angles)
    front_half = rope_pairs[..., :half_dim]
    back_half = rope_pairs[..., half_dim:]
    return jnp.concatenate(
        [front_half * cosine - back_half * sine_part, front_half * sine_part + back_half * cosine],
        axis=-1,
    )


def attend_slots(query_pack, latent_blocks, rope_blocks, slot_ids, table_flat, base_flat, lengths):
    sequences = query_pack.shape[0]
    span_blocks = table_flat.shape[0] // sequences
    block_rows = latent_blocks.shape[1]
    latent_width = latent_blocks.shape[2]
    flat_index = jnp.arange(table_flat.shape[0], dtype=jnp.int32)
    matches = table_flat[None, :] == slot_ids[:, None]
    owner_seq = jnp.sum(jnp.where(matches, (flat_index // span_blocks)[None, :], 0), axis=1)
    owner_base = jnp.sum(jnp.where(matches, base_flat[None, :], 0), axis=1)
    seq_hot = owner_seq[:, None] == jnp.arange(sequences, dtype=jnp.int32)[None, :]
    picked = jnp.einsum(
        "kb,bhc->khc", seq_hot.astype(jnp.bfloat16), query_pack, preferred_element_type=jnp.float32
    ).astype(jnp.bfloat16)
    scores = jnp.einsum(
        "khc,kpc->khp",
        picked[:, :, :latent_width],
        latent_blocks,
        preferred_element_type=jnp.float32,
    )
    scores = scores + jnp.einsum(
        "khr,krp->khp", picked[:, :, latent_width:], rope_blocks, preferred_element_type=jnp.float32
    )
    limits = jnp.sum(jnp.where(seq_hot, lengths[None, :], 0), axis=1)
    valid_mask = (
        owner_base[:, None] + jnp.arange(block_rows, dtype=jnp.int32)[None, :] < limits[:, None]
    )
    scores = jnp.where(valid_mask[:, None, :], scores, FLOOR_SCORE)
    slot_top = jnp.max(scores, axis=2)
    weights = jnp.where(valid_mask[:, None, :], jnp.exp(scores - slot_top[:, :, None]), 0.0)
    slot_total = jnp.sum(weights, axis=2)
    slot_mixed = jnp.einsum(
        "khp,kpc->khc",
        weights.astype(jnp.bfloat16),
        latent_blocks,
        preferred_element_type=jnp.float32,
    )
    seq_top = jnp.max(jnp.where(seq_hot[:, :, None], slot_top[:, None, :], FLOOR_SCORE), axis=0)
    top_at = jnp.sum(jnp.where(seq_hot[:, :, None], seq_top[None, :, :], 0.0), axis=1)
    factor = jnp.exp(slot_top - top_at)
    hot_wide = seq_hot.astype(jnp.float32)
    seq_total = jnp.einsum(
        "kb,kh->bh", hot_wide, slot_total * factor, precision=lax.Precision.HIGHEST
    )
    seq_mixed = jnp.einsum(
        "kb,khc->bhc", hot_wide, slot_mixed * factor[:, :, None], precision=lax.Precision.HIGHEST
    )
    return (seq_top, seq_total, seq_mixed)


def combine_parts(earlier, later):
    top_one, total_one, mixed_one = earlier
    top_two, total_two, mixed_two = later
    top_both = jnp.maximum(top_one, top_two)
    scale_two = jnp.exp(top_two - top_both)
    return (top_both, total_two * scale_two, mixed_two * scale_two[:, :, None])


def body(
    hidden_in,
    united_down,
    q_gain,
    kv_gain,
    q_up,
    key_up,
    value_up,
    latent_block_store,
    rope_pool,
    lengths,
    block_table,
):
    local_heads = key_up.shape[1] // NOPE
    span_blocks = block_table.shape[1]
    seq_index = lax.axis_index("seq")
    part_cols = jnp.dot(hidden_in, united_down, preferred_element_type=jnp.float32).astype(
        jnp.bfloat16
    )
    united_wide = lax.all_gather(part_cols, "tensor", axis=1, tiled=True).astype(jnp.float32)
    positions = lengths.astype(jnp.float32)
    query_latent = rms_scale(united_wide[:, :QR], q_gain).astype(jnp.bfloat16)
    new_latent = rms_scale(united_wide[:, QR : QR + LATENT_RANK], kv_gain).astype(jnp.bfloat16)
    new_rope = rotate_pairs(united_wide[:, QR + LATENT_RANK :], positions).astype(jnp.bfloat16)
    new_entry = jnp.concatenate([new_latent, new_rope], axis=1)
    row_count = q_up.shape[0]
    own_rows = lax.dynamic_slice_in_dim(query_latent, seq_index * row_count, row_count, 1)
    partial_query = jnp.dot(own_rows, q_up, preferred_element_type=jnp.float32)
    query_full = lax.psum(partial_query, "seq").reshape(B, local_heads, QH)
    query_nope = query_full[:, :, :NOPE].astype(jnp.bfloat16)
    key_heads = key_up.reshape(LATENT_RANK, local_heads, NOPE)
    score_scale = QH ** (-0.5)
    absorbed = jnp.einsum("bhn,khn->bhk", query_nope, key_heads, preferred_element_type=jnp.float32)
    query_lat = (absorbed * score_scale).astype(jnp.bfloat16)
    query_rot = (rotate_pairs(query_full[:, :, NOPE:], positions[:, None]) * score_scale).astype(
        jnp.bfloat16
    )
    query_pack = jnp.concatenate([query_lat, query_rot], axis=2)
    table_flat = block_table.reshape(-1)
    flat_index = jnp.arange(table_flat.shape[0], dtype=jnp.int32)
    base_flat = (seq_index * span_blocks + flat_index % span_blocks) * BLOCK_POSITIONS
    group_base = seq_index * (B * span_blocks)
    initial = (
        jnp.full((B, local_heads), FLOOR_SCORE, jnp.float32),
        jnp.zeros((B, local_heads), jnp.float32),
        jnp.zeros((B, local_heads, LATENT_RANK), jnp.float32),
    )
    latent_piece = lax.all_gather(latent_block_store, "tensor", axis=0, tiled=True)
    rope_piece = lax.all_gather(rope_pool, "tensor", axis=0, tiled=True)
    slot_ids = group_base + jnp.arange(latent_piece.shape[0], dtype=jnp.int32)
    fresh = attend_slots(
        query_pack, latent_piece, rope_piece, slot_ids, table_flat, base_flat, lengths
    )
    top_part, total_part, mixed_part = combine_parts(initial, fresh)
    grand_top = lax.pmax(top_part, "seq")
    factor = jnp.exp(top_part - grand_top)
    total_part, mixed_part = lax.psum((total_part * factor, mixed_part * factor[:, :, None]), "seq")
    top_part = grand_top
    own_score = jnp.sum(
        query_lat.astype(jnp.float32) * new_latent.astype(jnp.float32)[:, None, :], axis=2
    )
    own_score = own_score + jnp.sum(
        query_rot.astype(jnp.float32) * new_rope.astype(jnp.float32)[:, None, :], axis=2
    )
    final_top = jnp.maximum(top_part, own_score)
    old_scale = jnp.exp(top_part - final_top)
    own_weight = jnp.exp(own_score - final_top)
    totals = total_part * old_scale + own_weight
    mixture = mixed_part * old_scale[:, :, None]
    mixture = (
        mixture
        + own_weight.astype(jnp.bfloat16).astype(jnp.float32)[:, :, None]
        * new_latent.astype(jnp.float32)[:, None, :]
    )
    attended = (mixture / totals[:, :, None]).astype(jnp.bfloat16)
    value_heads = value_up.reshape(LATENT_RANK, local_heads, VD)
    attn_out = jnp.einsum("bhk,khv->bhv", attended, value_heads, preferred_element_type=jnp.float32)
    attn_out = attn_out.reshape(B, local_heads * VD).astype(jnp.bfloat16)
    return (attn_out, new_entry)


def solution(mesh):
    in_specs = (
        P(),
        P(None, "tensor"),
        P(),
        P(),
        P("seq", "tensor"),
        P(None, "tensor"),
        P(None, "tensor"),
        P(("seq", "tensor"), None, None),
        P(("seq", "tensor"), None, None),
        P(),
        P(None, "seq"),
    )
    out_specs = (P(None, "tensor"), P())
    return jax.shard_map(body, mesh=mesh, in_specs=in_specs, out_specs=out_specs, check_vma=False)
```

profile of v0, /device:TPU:0, one launch (start us, length us, event | category | flops | bytes accessed | tf_op | source)
XLA Modules:
  0.0 235.1 jit_solution(18055280222267351378)
XLA Ops:
  8.1 4.3 %fusion.37 = bf16[1,528,16]{1,2,0:T(8,128)(2,1)S(1)} fusion(bf16[16,5120]{1,0:T(8,128)(2,1)} %param.11, bf16[5120,528]{0,1:T(8,128)(2,1)} %param.12), kind=kOutput, calls=%fused_computation.22 | convolution fusion | flops 86515968 | bytes 5587456 | tf_op jit(solution)/shard_map/dot_general | solution.py:111
  12.3 6.3 %all-gather = bf16[4,528,16]{1,2,0:T(8,128)(2,1)S(1)} all-gather(bf16[1,528,16]{1,2,0:T(8,128)(2,1)S(1)} %fusion.37), channel_id=1, replica_groups=mesh['seq'=8,'tensor'=4] {'tensor'}, dimensions={0}, use_global_device_ids=true | all-gather | bytes 84480 | tf_op jit(solution)/shard_map/all_gather | solution.py:114
  18.7 0.1 reshape.217
  18.8 0.1 multiply_reduce_fusion.2
  18.9 0.8 dynamic-slice
  19.7 0.5 fusion.62
  20.2 0.2 reshape.212
  20.4 1.2 copy.83
  21.7 0.5 all-gather.6.cloned.1.call-update
  22.3 0.5 all-gather.4.cloned.1.call-update
  22.9 0.1 copy.81
  23.0 0.1 eq.34
  23.1 0.1 multiply_cosine_fusion
  23.3 0.1 maximum_convert_fusion
  23.3 0.1 multiply_reduce_fusion.3
  23.5 0.2 fusion.56
  23.6 0.1 select_reduce_fusion.2
  23.7 0.1 copy-done.7
  23.8 0.1 add_compare_fusion
  23.9 0.7 fusion.78
  24.6 71.6 %all-reduce.3.cloned.1.call-done = f32[16,32,192]{2,0,1:T(8,128)} async-done(((f32[16,32,192]{2,0,1:T(8,128)}), f32[16,32,192]{2,0,1:T(8,128)}) %all-reduce.3.cloned.1.call-update) | async-done | bytes 393232 | tf_op jit(solution)/shard_map/psum | solution.py:123
  96.2 1.2 multiply_subtract_fusion
  97.4 0.9 multiply_reduce_fusion.1
  98.2 4.2 %multiply_reduce_fusion = (f32[16,32]{0,1:T(8,128)}, bf16[16,32,512]{2,0,1:T(8,128)(2,1)S(1)}) fusion(f32[16,512]{1,0:T(8,128)S(1)} %get-tuple-element.8, f32[16,32,192]{2,0,1:T(8,128)} %all-reduce.3.cloned.1.call-done, bf16[512,4096]{1,0:T(8,128)(2,1)} %param.16), kind=kOutput, calls=%fused_computation.26 | convolution fusion | flops 68419072 | bytes 4884480 | tf_op jit(solution)/shard_map/bhn,khn->bhk/dot_general | solution.py:127
  102.4 0.9 convolution_convert_fusion
  103.3 1.6 slice.47
  104.9 0.1 slice.48
  105.0 2.7 %fusion.45 = f32[64,32,128]{2,1,0:T(8,128)} fusion(bf16[64,64,128]{2,1,0:T(8,128)(2,1)} %all-gather.6.cloned.1.call-done, bf16[64,32,64]{2,0,1:T(8,128)(2,1)S(1)} %slice.48), kind=kOutput, calls=%fused_computation.33 | convolution fusion | flops 33554432 | bytes 2359296 | tf_op jit(solution)/shard_map/khr,krp->khp/dot_general | solution.py:57
  107.7 6.7 %fusion.79 = (f32[64,32]{1,0:T(8,128)S(1)}, f32[64,32,128]{2,1,0:T(8,128)S(1)}) fusion(f32[64,32,128]{2,1,0:T(8,128)} %fusion.45, bf16[64,128,512]{2,1,0:T(8,128)(2,1)} %all-gather.4.cloned.1.call-done, bf16[64,32,512]{2,0,1:T(8,128)(2,1)} %slice.47, pred[64,128]{1,0:T(8,128)(4,1)S(1)} %add_compare_fusion), kind=kOutput, calls=%fused_computation.104 | convolution fusion | flops 269219840 | bytes 12599296 | tf_op jit(solution)/shard_map/khc,kpc->khp/dot_general | solution.py:51
  114.5 0.2 select_reduce_fusion.1
  114.6 0.1 select_reduce_fusion
  114.8 20.1 %pmax.7 = f32[16,32]{1,0:T(8,128)S(1)} all-reduce(f32[16,32]{1,0:T(8,128)S(1)} %broadcast_maximum_fusion), channel_id=1, replica_groups=mesh['seq'=8,'tensor'=4] {'seq'}, use_global_device_ids=true, to_apply=%region_8.9 | all-reduce | flops 512 | bytes 4096 | tf_op jit(solution)/shard_map/pmax | solution.py:149
  134.9 0.6 subtract_exponential_fusion.2
  135.5 0.1 copy.88
  135.6 1.4 copy.90
  137.0 1.4 copy.91
  138.4 4.3 %convolution_multiply_fusion = f32[64,32,512]{2,1,0:T(8,128)S(1)} fusion(bf16[64,128,512]{2,1,0:T(8,128)(2,1)} %all-gather.4.cloned.1.call-done, f32[64,32]{1,0:T(8,128)S(1)} %subtract_exponential_fusion, f32[64,32,128]{2,1,0:T(8,128)S(1)} %get-tuple-element.24, f32[64,32]{1,0:T(8,128)S(1)} %get-tuple-element.23, pred[64,128]{1,0:T(8,128)(4,1)S(1)} %add_compare_fusion), kind=kOutput, calls=%fused_computation.8 | convolution fusion | flops 270270464 | bytes 13656064 | tf_op jit(solution)/shard_map/khp,kpc->khc/dot_general | solution.py:68
  142.7 4.9 %fusion.19 = f32[16,32,512]{2,0,1:T(8,128)} fusion(f32[64,32,512]{2,1,0:T(8,128)S(1)} %convolution_multiply_fusion, f32[16,32]{0,1:T(8,128)S(1)} %copy-done.6, f32[16,32]{0,1:T(8,128)S(1)} %copy-done.5, s32[64]{0:T(128)S(1)} %copy-done.10), kind=kOutput, calls=%fused_computation.15 | convolution fusion | flops 201851904 | bytes 5247232 | tf_op jit(solution)/shard_map/kb,khc->bhc/dot_general | solution.py:81
  147.6 1.4 pad_maximum_fusion
  149.0 1.4 copy.93
  150.4 0.7 copy.92
  151.1 0.6 fusion.39
  151.7 0.8 fusion.38
  152.5 17.8 %psum.23 = f32[16,32]{1,0:T(8,128)S(1)} all-reduce(f32[16,32]{1,0:T(8,128)S(1)} %fusion.38), channel_id=1, replica_groups=mesh['seq'=8,'tensor'=4] {'seq'}, use_global_device_ids=true, to_apply=%region_14.15 | all-reduce | flops 512 | bytes 4096 | tf_op jit(solution)/shard_map/psum | solution.py:151
  170.3 0.7 multiply_add_fusion.1
  171.3 52.3 %all-reduce.5.cloned.1.call-done = f32[16,32,512]{2,0,1:T(8,128)} async-done(((f32[16,32,512]{2,0,1:T(8,128)}), f32[16,32,512]{2,0,1:T(8,128)}) %all-reduce.5.cloned.1.call-update) | async-done | bytes 1048592 | tf_op jit(solution)/shard_map/psum | solution.py:151
  223.5 3.5 %fusion.34 = bf16[32,2,8,128]{3,2,1,0:T(8,128)(2,1)S(1)} fusion(f32[16,32,512]{2,0,1:T(8,128)} %all-reduce.5.cloned.1.call-done, f32[16,32]{0,1:T(8,128)S(1)} %copy.96, f32[16,32]{0,1:T(8,128)S(1)} %copy.95, f32[16,32]{0,1:T(8,128)S(1)} %copy.94, f32[16,512]{1,0:T(8,128)S(1)} %get-tuple-element.8, bf16[512,4096]{1,0:T(8,128)(2,1)} %param.17), kind=kOutput, calls=%fused_computation.20 | convolution fusion | flops 68485120 | bytes 5412864 | tf_op jit(solution)/shard_map/bhk,khv->bhv/dot_general | solution.py:171
  227.0 0.7 copy.139
  (49 shorter events, 0.7 us)
Async XLA Ops:
  8.0 11.7 %copy-start = (bf16[192,6144]{1,0:T(8,128)(2,1)S(1)}, bf16[192,6144]{1,0:T(8,128)(2,1)}, u32[]{:S(2)}) copy-start(bf16[192,6144]{1,0:T(8,128)(2,1)} %param.15) | copy-start | bytes 7077892
  8.0 88.2 %all-reduce.3.cloned.1.call-start = ((), (), s32[]{:S(2)}) async-start(), calls=%async_computation | async-start | bytes 1048576 | tf_op jit(solution)/shard_map/psum | solution.py:123
  18.6 4.2 %copy-start.13 = (s32[16]{0:T(128)S(1)}, s32[16]{0:T(128)}, u32[]{:S(2)}) copy-start(s32[16]{0:T(128)} %param.20) | copy-start | bytes 196
  18.6 4.3 %copy-start.11 = (s32[16,4]{0,1:T(4,128)S(1)}, s32[16,4]{0,1:T(4,128)}, u32[]{:S(2)}) copy-start(s32[16,4]{0,1:T(4,128)} %param.21) | copy-start | bytes 772
  18.7 5.3 %copy-start.12 = (f32[512]{0:T(512)S(1)}, f32[512]{0:T(512)}, u32[]{:S(2)}) copy-start(f32[512]{0:T(512)} %param.14) | copy-start | bytes 6148
  21.6 83.4 %all-gather.6.cloned.1.call-start = ((), (), s32[]{:S(2)}) async-start(), calls=%async_computation.2 | async-start | bytes 1310720 | tf_op jit(solution)/shard_map/all_gather | solution.py:143
  22.2 85.5 %all-gather.4.cloned.1.call-start = ((), (), s32[]{:S(2)}) async-start(), calls=%async_computation.1 | async-start | bytes 10485760 | tf_op jit(solution)/shard_map/all_gather | solution.py:142
  22.8 200.7 %all-reduce.5.cloned.1.call-start = ((), (), s32[]{:S(2)}) async-start(), calls=%async_computation.3 | async-start | bytes 2097152 | tf_op jit(solution)/shard_map/psum | solution.py:151
  23.2 0.6 copy-start.7
  23.2 0.7 copy-start.8
  23.6 79.7 %copy-start.9 = (s32[64]{0:T(128)}, s32[64]{0:T(128)S(1)}, u32[]{:S(2)}) copy-start(s32[64]{0:T(128)S(1)} %get-tuple-element.3) | copy-start | bytes 772
  134.9 0.6 copy-start.1
  138.3 4.3 %copy-start.5 = (f32[16,32]{0,1:T(8,128)S(1)}, f32[16,32]{0,1:T(8,128)}, u32[]{:S(2)}) copy-start(f32[16,32]{0,1:T(8,128)} %copy.90) | copy-start | bytes 6148
  138.3 4.3 %copy-start.6 = (f32[16,32]{0,1:T(8,128)S(1)}, f32[16,32]{0,1:T(8,128)}, u32[]{:S(2)}) copy-start(f32[16,32]{0,1:T(8,128)} %copy.91) | copy-start | bytes 6148
  138.3 4.3 %copy-start.10 = (s32[64]{0:T(128)S(1)}, s32[64]{0:T(128)}, u32[]{:S(2)}) copy-start(s32[64]{0:T(128)} %copy-done.9) | copy-start | bytes 772
  142.6 7.8 %copy-start.4 = (f32[16,32]{0,1:T(8,128)S(1)}, f32[16,32]{0,1:T(8,128)}, u32[]{:S(2)}) copy-start(f32[16,32]{0,1:T(8,128)} %get-tuple-element.25) | copy-start | bytes 6148
  142.7 9.1 %copy-start.3 = (f32[16,32]{1,0:T(8,128)S(1)}, f32[16,32]{1,0:T(8,128)}, u32[]{:S(2)}) copy-start(f32[16,32]{1,0:T(8,128)} %get-tuple-element.18) | copy-start | bytes 6148
  142.7 27.6 %copy-start.2 = (f32[16,32]{1,0:T(8,128)S(1)}, f32[16,32]{1,0:T(8,128)}, u32[]{:S(2)}) copy-start(f32[16,32]{1,0:T(8,128)} %copy-done.1) | copy-start | bytes 6148
Sparse Core Ops, SparseCore 0:
  21.8 74.3 all-reduce.2
  147.7 75.7 all-reduce.4
Sparse Core Ops, SparseCore 1:
  23.7 18.3 all-gather.5
  43.4 58.1 all-gather.3
where the time goes:
time: 236 us; the launch traced here: 235 us
  waiting for transfers between devices  125 us (53%)
  blocking collectives  44.2 us (19%)
  matrix products  32.6 us (14%)
  between operations  15.8 us (7%)
  local copies, waits for them, and re-layouts  10.2 us (4%)
  other arithmetic  7.24 us (3%)
    psum x1, waiting for transfers between devices, body(): query_full = lax.psum(partial_query, 'seq').reshape(B, local_heads, QH)  71.6 us
    psum x1, waiting for transfers between devices, body(): lax.psum((total_part * factor, mixed_part * factor[:, :, None]), 'seq')  52.3 us
    pmax x1, blocking collectives, body(): grand_top = lax.pmax(top_part, 'seq')  20.1 us
    psum x1, blocking collectives, body(): lax.psum((total_part * factor, mixed_part * factor[:, :, None]), 'seq')  17.8 us
    dot_general x1, matrix products, attend_slots(): jnp.einsum('khc,kpc->khp', picked[:, :, :latent_width], latent_blocks, pr...  6.66 us
    all_gather x1, blocking collectives, body(): lax.all_gather(part_cols, 'tensor', axis=1, tiled=True).astype(jnp.float32)  6.27 us
    dot_general x1, matrix products, attend_slots(): jnp.einsum('kb,khc->bhc', hot_wide, slot_mixed * factor[:, :, None], prec...  4.91 us
  transfers between devices with their start and end apart: 4, of which 2 were waited for; matrix products, arithmetic and copies ran while one was open for 8% of the time, Pallas kernels for 0%

commit v1 on v0

--- a/solution.py
+++ b/solution.py
@@ -120,7 +120,7 @@
     row_count = q_up.shape[0]
     own_rows = lax.dynamic_slice_in_dim(query_latent, seq_index * row_count, row_count, 1)
     partial_query = jnp.dot(own_rows, q_up, preferred_element_type=jnp.float32)
-    query_full = lax.psum(partial_query, "seq").reshape(B, local_heads, QH)
+    query_full = jnp.sum(lax.all_gather(partial_query, "seq"), axis=0).reshape(B, local_heads, QH)
     query_nope = query_full[:, :, :NOPE].astype(jnp.bfloat16)
     key_heads = key_up.reshape(LATENT_RANK, local_heads, NOPE)
     score_scale = QH ** (-0.5)

time: 236 us -> 285 us (1.21)
  waiting for transfers between devices: 125 us -> 178 us
  local copies, waits for them, and re-layouts: 10.2 us -> 6.08 us
    psum x1 -> x0, waiting for transfers between devices: 71.6 us -> none  [body(): query_full = lax.psum(partial_query, 'seq').reshape(B, local_heads, QH)]
    all_gather x0 -> x1, waiting for transfers between devices: none -> 58.6 us  [body(): lax.all_gather(partial_query, 'seq')]
    all_gather x1, waiting for transfers between devices: 0.01 us -> 57.2 us  [body(): lax.all_gather(latent_block_store, 'tensor', axis=0, tiled=True)]
    all_gather x1, waiting for transfers between devices: 0.03 us -> 7.23 us  [body(): rope_piece = lax.all_gather(rope_pool, 'tensor', axis=0, tiled=True)]
  transfers between devices with their start and end apart: 4 -> 4, of which waited for: 2 -> 4; matrix products, arithmetic and copies ran while one was open for 8% -> 6% of each run, Pallas kernels for 0% -> 0%
where the time goes in v1:
time: 285 us; the launch traced here: 284 us
  waiting for transfers between devices  178 us (62%)
  blocking collectives  45.9 us (16%)
  matrix products  33.2 us (12%)
  between operations  14 us (5%)
  other arithmetic  7.12 us (2%)
  local copies, waits for them, and re-layouts  6.08 us (2%)
    all_gather x1, waiting for transfers between devices, body(): lax.all_gather(partial_query, 'seq')  58.6 us
    all_gather x1, waiting for transfers between devices, body(): lax.all_gather(latent_block_store, 'tensor', axis=0, tiled=True)  57.2 us
    psum x1, waiting for transfers between devices, body(): lax.psum((total_part * factor, mixed_part * factor[:, :, None]), 'seq')  53.3 us
    pmax x1, blocking collectives, body(): grand_top = lax.pmax(top_part, 'seq')  21.8 us
    psum x1, blocking collectives, body(): lax.psum((total_part * factor, mixed_part * factor[:, :, None]), 'seq')  17.7 us
    all_gather x1, waiting for transfers between devices, body(): rope_piece = lax.all_gather(rope_pool, 'tensor', axis=0, tiled=True)  7.23 us
    dot_general x1, matrix products, attend_slots(): jnp.einsum('khc,kpc->khp', picked[:, :, :latent_width], latent_blocks, pr...  6.66 us
    all_gather x1, blocking collectives, body(): lax.all_gather(part_cols, 'tensor', axis=1, tiled=True).astype(jnp.float32)  6.4 us
  transfers between devices with their start and end apart: 4, of which 4 were waited for; matrix products, arithmetic and copies ran while one was open for 6% of the time, Pallas kernels for 0%

profile of v1, /device:TPU:0, one launch (start us, length us, event | category | flops | bytes accessed | tf_op | source)
XLA Modules:
  0.0 284.2 jit_solution(3028122637483291262)
XLA Ops:
  7.2 4.3 %fusion.37 = bf16[1,528,16]{1,2,0:T(8,128)(2,1)S(1)} fusion(bf16[16,5120]{1,0:T(8,128)(2,1)} %param.11, bf16[5120,528]{0,1:T(8,128)(2,1)} %param.12), kind=kOutput, calls=%fused_computation.22 | convolution fusion | flops 86515968 | bytes 5587456 | tf_op jit(solution)/shard_map/dot_general | solution.py:111
  11.5 6.4 %all-gather.1 = bf16[4,528,16]{1,2,0:T(8,128)(2,1)S(1)} all-gather(bf16[1,528,16]{1,2,0:T(8,128)(2,1)S(1)} %fusion.37), channel_id=1, replica_groups=mesh['seq'=8,'tensor'=4] {'tensor'}, dimensions={0}, use_global_device_ids=true | all-gather | bytes 84480 | tf_op jit(solution)/shard_map/all_gather | solution.py:114
  18.0 0.1 reshape.218
  18.1 0.1 multiply_reduce_fusion.2
  18.3 0.8 dynamic-slice
  19.0 1.2 fusion.62
  20.4 0.7 all-gather.8.cloned.1.call-update
  21.1 0.7 all-gather.6.cloned.1.call-update
  21.9 0.1 copy.88
  22.0 0.1 eq.34
  22.1 0.1 multiply_cosine_fusion
  22.2 0.1 maximum_convert_fusion
  22.3 0.1 multiply_reduce_fusion.3
  22.4 0.2 fusion.56
  22.6 0.1 select_reduce_fusion.2
  22.7 0.1 copy-done.1
  22.8 0.1 add_compare_fusion
  22.9 0.7 fusion.78
  23.6 58.6 %all-gather.10.cloned.1.call-done = f32[128,6144]{1,0:T(8,128)} async-done(((f32[16,6144]{1,0:T(8,128)}), f32[128,6144]{1,0:T(8,128)}) %all-gather.10.cloned.1.call-update) | async-done | bytes 3145744 | tf_op jit(solution)/shard_map/all_gather | solution.py:123
  82.2 2.1 reduce_sum.94
  84.3 0.2 reshape.212
  84.6 0.1 fusion.79
  84.7 0.3 multiply_subtract_fusion
  85.0 0.2 multiply_reduce_fusion.1
  85.3 4.1 %multiply_reduce_fusion = (f32[16,32]{0,1:T(8,128)}, bf16[16,32,512]{2,0,1:T(8,128)(2,1)S(1)}) fusion(f32[16,512]{1,0:T(8,128)S(1)} %get-tuple-element.8, bf16[16,32,128]{2,1,0:T(8,128)(2,1)S(1)} %slice.44, bf16[512,4096]{1,0:T(8,128)(2,1)} %param.16), kind=kOutput, calls=%fused_computation.26 | convolution fusion | flops 68419072 | bytes 4884480 | tf_op jit(solution)/shard_map/bhn,khn->bhk/dot_general | solution.py:127
  89.4 0.9 convolution_convert_fusion
  90.3 1.6 slice.47
  91.8 0.1 slice.48
  91.9 7.2 %all-gather.8.cloned.1.call-done = bf16[64,64,128]{2,1,0:T(8,128)(2,1)} async-done(((bf16[16,64,128]{2,1,0:T(8,128)(2,1)}), bf16[64,64,128]{2,1,0:T(8,128)(2,1)}) %all-gather.8.cloned.1.call-update) | async-done | bytes 1048592 | tf_op jit(solution)/shard_map/all_gather | solution.py:143
  99.2 2.7 fusion.45
  101.9 57.2 %all-gather.6.cloned.1.call-done = bf16[64,128,512]{2,1,0:T(8,128)(2,1)} async-done(((bf16[16,128,512]{2,1,0:T(8,128)(2,1)}), bf16[64,128,512]{2,1,0:T(8,128)(2,1)}) %all-gather.6.cloned.1.call-update) | async-done | bytes 8388624 | tf_op jit(solution)/shard_map/all_gather | solution.py:142
  159.0 6.7 %fusion.80 = (f32[64,32]{1,0:T(8,128)S(1)}, f32[64,32,128]{2,1,0:T(8,128)S(1)}) fusion(f32[64,32,128]{2,1,0:T(8,128)} %fusion.45, bf16[64,128,512]{2,1,0:T(8,128)(2,1)} %all-gather.6.cloned.1.call-done, bf16[64,32,512]{2,0,1:T(8,128)(2,1)} %slice.47, pred[64,128]{1,0:T(8,128)(4,1)S(1)} %add_compare_fusion), kind=kOutput, calls=%fused_computation.105 | convolution fusion | flops 269219840 | bytes 12599296 | tf_op jit(solution)/shard_map/khc,kpc->khp/dot_general | solution.py:51
  165.8 0.2 select_reduce_fusion.1
  165.9 0.1 select_reduce_fusion
  166.1 21.8 %pmax.7 = f32[16,32]{1,0:T(8,128)S(1)} all-reduce(f32[16,32]{1,0:T(8,128)S(1)} %broadcast_maximum_fusion), channel_id=1, replica_groups=mesh['seq'=8,'tensor'=4] {'seq'}, use_global_device_ids=true, to_apply=%region_8.9 | all-reduce | flops 512 | bytes 4096 | tf_op jit(solution)/shard_map/pmax | solution.py:149
  187.9 0.6 subtract_exponential_fusion.2
  188.5 0.1 copy.97
  188.7 0.8 copy.99
  189.4 4.2 %convolution_multiply_fusion = f32[64,32,512]{2,1,0:T(8,128)S(1)} fusion(bf16[64,128,512]{2,1,0:T(8,128)(2,1)} %all-gather.6.cloned.1.call-done, f32[64,32]{1,0:T(8,128)S(1)} %subtract_exponential_fusion, f32[64,32,128]{2,1,0:T(8,128)S(1)} %get-tuple-element.26, f32[64,32]{1,0:T(8,128)S(1)} %get-tuple-element.25, pred[64,128]{1,0:T(8,128)(4,1)S(1)} %add_compare_fusion), kind=kOutput, calls=%fused_computation.8 | convolution fusion | flops 270270464 | bytes 13656064 | tf_op jit(solution)/shard_map/khp,kpc->khc/dot_general | solution.py:68
  193.7 4.9 %fusion.19 = f32[16,32,512]{2,0,1:T(8,128)} fusion(f32[64,32,512]{2,1,0:T(8,128)S(1)} %convolution_multiply_fusion, f32[16,32]{0,1:T(8,128)S(1)} %copy.100, f32[16,32]{0,1:T(8,128)S(1)} %copy.99, s32[64]{0:T(128)S(1)} %copy-done.5), kind=kOutput, calls=%fused_computation.15 | convolution fusion | flops 201851904 | bytes 5247232 | tf_op jit(solution)/shard_map/kb,khc->bhc/dot_general | solution.py:81
  198.6 1.4 pad_maximum_fusion
  200.1 0.8 copy.101
  200.9 0.6 fusion.39
  201.5 0.7 fusion.38
  202.3 17.7 %psum.15 = f32[16,32]{1,0:T(8,128)S(1)} all-reduce(f32[16,32]{1,0:T(8,128)S(1)} %fusion.38), channel_id=1, replica_groups=mesh['seq'=8,'tensor'=4] {'seq'}, use_global_device_ids=true, to_apply=%region_14.15 | all-reduce | flops 512 | bytes 4096 | tf_op jit(solution)/shard_map/psum | solution.py:151
  220.2 53.3 %all-reduce.2.cloned.1.call-done = f32[16,32,512]{2,0,1:T(8,128)} async-done(((f32[16,32,512]{2,0,1:T(8,128)}), f32[16,32,512]{2,0,1:T(8,128)}) %all-reduce.2.cloned.1.call-update) | async-done | bytes 1048592 | tf_op jit(solution)/shard_map/psum | solution.py:151
  273.5 3.5 %fusion.34 = bf16[32,2,8,128]{3,2,1,0:T(8,128)(2,1)S(1)} fusion(f32[16,32,512]{2,0,1:T(8,128)} %all-reduce.2.cloned.1.call-done, f32[16,32]{0,1:T(8,128)S(1)} %copy.105, f32[16,32]{0,1:T(8,128)S(1)} %copy.104, f32[16,32]{0,1:T(8,128)S(1)} %copy.103, f32[16,512]{1,0:T(8,128)} %copy-done.3, bf16[512,4096]{1,0:T(8,128)(2,1)} %param.17), kind=kOutput, calls=%fused_computation.20 | convolution fusion | flops 68485120 | bytes 5412864 | tf_op jit(solution)/shard_map/bhk,khv->bhv/dot_general | solution.py:171
  277.0 0.7 copy.159
  (41 shorter events, 0.8 us)
Async XLA Ops:
  7.2 11.9 %copy-start = (bf16[192,6144]{1,0:T(8,128)(2,1)S(1)}, bf16[192,6144]{1,0:T(8,128)(2,1)}, u32[]{:S(2)}) copy-start(bf16[192,6144]{1,0:T(8,128)(2,1)} %param.15) | copy-start | bytes 7077892
  7.2 75.0 %all-gather.10.cloned.1.call-start = ((), (), s32[]{:S(2)}) async-start(), calls=%async_computation.3 | async-start | bytes 3538944 | tf_op jit(solution)/shard_map/all_gather | solution.py:123
  11.5 10.3 %copy-start.8 = (s32[16]{0:T(128)S(1)}, s32[16]{0:T(128)}, u32[]{:S(2)}) copy-start(s32[16]{0:T(128)} %param.20) | copy-start | bytes 196
  11.5 10.3 %copy-start.6 = (s32[16,4]{0,1:T(4,128)S(1)}, s32[16,4]{0,1:T(4,128)}, u32[]{:S(2)}) copy-start(s32[16,4]{0,1:T(4,128)} %param.21) | copy-start | bytes 772
  11.5 11.4 %copy-start.7 = (f32[512]{0:T(512)S(1)}, f32[512]{0:T(512)}, u32[]{:S(2)}) copy-start(f32[512]{0:T(512)} %param.14) | copy-start | bytes 6148
  20.3 78.9 %all-gather.8.cloned.1.call-start = ((), (), s32[]{:S(2)}) async-start(), calls=%async_computation.1 | async-start | bytes 1310720 | tf_op jit(solution)/shard_map/all_gather | solution.py:143
  21.1 138.0 %all-gather.6.cloned.1.call-start = ((), (), s32[]{:S(2)}) async-start(), calls=%async_computation | async-start | bytes 10485760 | tf_op jit(solution)/shard_map/all_gather | solution.py:142
  21.8 251.7 %all-reduce.2.cloned.1.call-start = ((), (), s32[]{:S(2)}) async-start(), calls=%async_computation.2 | async-start | bytes 2097152 | tf_op jit(solution)/shard_map/psum | solution.py:151
  22.2 0.6 copy-start.1
  22.2 0.6 copy-start.2
  22.6 66.8 %copy-start.4 = (s32[64]{0:T(128)}, s32[64]{0:T(128)S(1)}, u32[]{:S(2)}) copy-start(s32[64]{0:T(128)S(1)} %get-tuple-element.3) | copy-start | bytes 772
  23.6 65.8 %copy-start.3 = (f32[16,512]{1,0:T(8,128)}, f32[16,512]{1,0:T(8,128)S(1)}, u32[]{:S(2)}) copy-start(f32[16,512]{1,0:T(8,128)S(1)} %get-tuple-element.8) | copy-start | bytes 98308
  189.4 4.2 %copy-start.5 = (s32[64]{0:T(128)S(1)}, s32[64]{0:T(128)}, u32[]{:S(2)}) copy-start(s32[64]{0:T(128)} %copy-done.4) | copy-start | bytes 772
Sparse Core Ops, SparseCore 0:
  20.4 61.7 all-gather.9
  83.8 15.3 all-gather.7
  100.7 58.2 all-gather.5
  198.7 74.7 all-reduce.1
